TPU v7x, 32 devices: a whole 2x2x4 slice. The times are simulated.
32 devices in a mesh: dp: 4 (over x, y), sp: 8 (over z, core).
Axes of the slice: x: 2, y: 2, z: 4, core: 2. Of those that a mesh axis runs over, the one named last changes fastest.
Arguments:
- q: bfloat16 [128, 96, 192], P('dp'), parts along dimension 0
- k: bfloat16 [128, 4096, 8, 192], P('dp', 'sp'), parts along dimension 0
- v: bfloat16 [128, 4096, 8, 192], P('dp', 'sp'), parts along dimension 0
Outputs:
- q: bfloat16 [128, 96, 192], P('dp'), parts along dimension 0
There are 4 independent parts. A program takes and returns all parts, laid end to end along the dimension named above; each array names one.
All inputs are finite; a program needn't handle non-finite values.
Results may differ from a plain program's by a relative error of at most 0.012.
Values are sent between devices in bfloat16 or wider.
A program may use at most 2 GiB of HBM per device.

v0:
```python
import jax
import jax.numpy as jnp
from jax import lax
from jax.sharding import PartitionSpec as P


def einsum(form, a, b):
    return jnp.einsum(form, a.astype(jnp.float32), b.astype(jnp.float32))


def part_of(q, k, v):
    grouped = q.reshape(q.shape[0], k.shape[2], -1, q.shape[2])
    scores = einsum("bgsd,bugd->bgsu", grouped, k) * q.shape[2] ** -0.5
    high = jnp.max(scores, -1, keepdims=True)
    weights = jnp.exp(scores - high)
    seen = einsum("bgsu,bugd->bgsd", weights.astype(jnp.bfloat16), v)
    return jnp.concatenate([seen, jnp.sum(weights, -1, keepdims=True), high], -1)


def together(parts):
    seen, total, high = parts[..., :-2], parts[..., -2:-1], parts[..., -1:]
    scale = jnp.exp(high - jnp.max(high, 0))
    return (jnp.sum(seen * scale, 0) / jnp.sum(total * scale, 0)).astype(jnp.bfloat16)


def solution(mesh):
    def step(q, k, v):
        return together(lax.all_gather(part_of(q, k, v), "sp")).reshape(q.shape)

    return jax.shard_map(
        step,
        mesh=mesh,
        in_specs=(P("dp", None, None), P("dp", "sp", None, None), P("dp", "sp", None, None)),
        out_specs=P("dp", None, None),
        check_vma=False,
    )
```

profile of v0, /device:TPU:0, one launch (start us, length us, event | category | flops | bytes accessed | tf_op | source)
XLA Modules:
  0.0 357.1 jit_solution(14648562576572566807)
XLA Ops:
  6.5 0.0 all-gather.3.cloned.1.call-start
  6.5 2.3 copy.38
  8.8 17.8 %multiply_reduce_fusion = (f32[32,8,12]{2,1,0:T(8,128)S(1)}, f32[32,8,12,512]{3,2,1,0:T(8,128)S(1)}) fusion(bf16[32,512,8,192]{1,3,2,0:T(8,128)(2,1)} %param.4, bf16[32,8,12,192]{3,0,2,1:T(8,128)(2,1)S(1)} %bitcast.16), kind=kOutput, calls=%fused_computation.3 | convolution fusion | flops 607122432 | bytes 57815040 | tf_op jit(solution)/shard_map/bgsd,bugd->bgsu/dot_general | solution.py:8
  26.7 0.0 copy-start
  26.7 3.2 copy-done
  29.9 2.2 fusion.1
  32.2 23.8 %fusion.3 = f32[32,8,12,192]{3,2,1,0:T(8,128)} fusion(bf16[32,512,8,192]{1,3,2,0:T(8,128)(2,1)} %param.5, f32[32,8,12,512]{3,2,1,0:T(8,128)} %copy-done, f32[32,8,12]{2,1,0:T(8,128)S(1)} %get-tuple-element.10), kind=kOutput, calls=%fused_computation.6 | convolution fusion | flops 608698368 | bytes 58994688 | tf_op jit(solution)/shard_map/bgsu,bugd->bgsd/dot_general | solution.py:8
  56.0 1.7 copy.42
  57.6 3.0 copy.43
  60.7 4.1 %pad_maximum_fusion = f32[32,8,12,194]{3,2,1,0:T(8,128)S(1)} fusion(f32[32,8,12,1]{3,2,1,0:T(8,128)} %copy.43, f32[32,8,12,1]{3,2,1,0:T(8,128)S(1)} %copy.42, f32[32,8,12,192]{3,2,1,0:T(8,128)} %fusion.3), kind=kLoop, calls=%fused_computation.7 | loop fusion | flops 1191936 | bytes 4767744 | tf_op jit(solution)/shard_map/concatenate | solution.py:17
  64.8 4.6 %copy.44 = f32[32,8,12,194]{3,1,2,0:T(8,128)} copy(f32[32,8,12,194]{3,2,1,0:T(8,128)S(1)} %pad_maximum_fusion) | data formatting | bytes 4767744 | tf_op jit(solution)/shard_map/concatenate | solution.py:17
  69.4 0.0 all-gather.3.cloned.1.call-update
  69.4 223.2 %all-gather.3.cloned.1.call-done = f32[256,8,12,194]{3,1,2,0:T(8,128)} async-done(((f32[32,8,12,194]{3,1,2,0:T(8,128)}), f32[256,8,12,194]{3,1,2,0:T(8,128)}) %all-gather.3.cloned.1.call-update) | async-done | bytes 19070992 | tf_op jit(solution)/shard_map/all_gather | solution.py:28
  292.7 23.3 %fusion.12 = (f32[8,32,8,12,1]{4,2,3,1,0:T(8,128)}, f32[32,8,12]{1,2,0:T(8,128)S(1)}, f32[8,32,8,12,1]{4,2,3,1,0:T(8,128)}) fusion(f32[8,32,8,12,194]{4,2,3,1,0:T(8,128)} %bitcast.14), kind=kLoop, calls=%fused_computation.19 | loop fusion | flops 21504 | bytes 405504 | tf_op jit(solution)/shard_map/slice | solution.py:21
  316.0 9.1 %copy.58 = f32[8,32,8,12,1]{1,2,4,3,0:T(8,128)S(1)} copy(f32[8,32,8,12,1]{4,2,3,1,0:T(8,128)} %get-tuple-element.5) | data formatting | bytes 196608
  325.1 0.1 copy.60
  325.2 9.1 %copy.57 = f32[8,32,8,12,1]{1,2,4,3,0:T(8,128)S(1)} copy(f32[8,32,8,12,1]{4,2,3,1,0:T(8,128)} %get-tuple-element.7) | data formatting | bytes 196608
  334.4 0.1 multiply_reduce_fusion.1
  334.5 0.9 copy.46
  335.4 10.6 %fusion = f32[32,8,12,192]{3,1,2,0:T(8,128)S(1)} fusion(f32[8,32,8,12,194]{4,2,3,1,0:T(8,128)} %bitcast.15, f32[8,32,8,12]{2,3,1,0:T(8,128)S(1)} %copy.46), kind=kLoop, calls=%fused_computation.1 | loop fusion | flops 8847360 | bytes 21331968 | tf_op jit(solution)/shard_map/reduce_sum | solution.py:23
  345.9 1.8 copy.48
  347.8 0.5 fusion.7
  348.3 2.0 copy.51
  (2 shorter events, 0.0 us)
Async XLA Ops:
  6.5 286.1 %all-gather.3.cloned.1.call-start = ((), (), s32[]{:S(2)}) async-start(), calls=%async_computation | async-start | bytes 28311552 | tf_op jit(solution)/shard_map/all_gather | solution.py:28
  26.7 3.2 copy-start
Sparse Core Ops, SparseCore 0:
  69.6 223.0 all-gather.2
where the time goes:
time: 358 us; the launch traced here: 357 us
  waiting for transfers between devices  223 us (62%)
  matrix products  41.7 us (12%)
  other arithmetic  40.8 us (11%)
  local copies, waits for them, and re-layouts  37.9 us (11%)
  between operations  13.5 us (4%)
    all_gather x1, waiting for transfers between devices, step(): return together(lax.all_gather(part_of(q, k, v), 'sp')).reshape(q.shape)  223 us
    dot_general x2, matrix products, einsum(): return jnp.einsum(form, a.astype(jnp.float32), b.astype(jnp.float32))  41.7 us
    unnamed x6, local copies, waits for them, and re-layouts  23.9 us
    slice x1, other arithmetic, together(): seen, total, high = (parts[..., :-2], parts[..., -2:-1], parts[..., -1:])  23.3 us
    reduce_sum x1, other arithmetic, together(): jnp.sum(seen * scale, 0) / jnp.sum(total * scale, 0)  10.6 us
  transfers between devices with their start and end apart: 1, of which 1 were waited for; matrix products, arithmetic and copies ran while one was open for 0% of the time, Pallas kernels for 0%

commit v1 on v0

v1 whole, which is shorter than its diff:
```python
import functools
import math

import jax
import jax.numpy as jnp
from jax import lax
from jax.experimental import pallas as pl
from jax.experimental.pallas import tpu as pltpu
from jax.sharding import PartitionSpec as P

F32, BF16 = jnp.float32, jnp.bfloat16
HEAD = 192
SHARE = 12
ROWS = 4 * SHARE
WIDE = 4 * HEAD
RATE = HEAD**-0.5 * math.log2(math.e)
PACK = 72
BATCH = 4
LEAD = 12
DEPTH = 6
HOP = dict(chip=2, outer=7, middle=12, last=17, out=20)
MESH = pl.DeviceIdType.MESH


def lanes(shape):
    return lax.broadcasted_iota(jnp.int32, shape, 1)


def rows(shape):
    return lax.broadcasted_iota(jnp.int32, shape, 0)


def spread(q):
    q = jnp.concatenate([q.astype(F32), jnp.zeros((ROWS, 256 - HEAD), F32)], 1)
    a, b = q[:, :128], q[:, 128:]
    ra, rb = pltpu.roll(a, 64, 1), pltpu.roll(b, 64, 1)
    low, head = lanes(a.shape) < 64, rows(a.shape) // SHARE
    x1, x2 = jnp.where(low, b, ra), jnp.where(low, ra, rb)
    tiles = []
    for first in (0, 2):
        tiles.append(jnp.where(head == first, a, 0.0))
        tiles.append(jnp.where(head == jnp.where(low, first, first + 1), x1, 0.0))
        tiles.append(jnp.where(head == first + 1, x2, 0.0))
    return jnp.concatenate(tiles, 1).astype(BF16)


def fold(o):
    t = [o[:, 128 * i : 128 * (i + 1)] for i in range(6)]
    low, head = lanes(t[0].shape) < 64, rows(t[0].shape) // SHARE
    lo = jnp.where(
        head == 0,
        t[0],
        jnp.where(
            head == 1,
            pltpu.roll(jnp.where(low, t[2], t[1]), 64, 1),
            jnp.where(head == 2, t[3], pltpu.roll(jnp.where(low, t[5], t[4]), 64, 1)),
        ),
    )
    half = ROWS // 2
    upper = jnp.where(head[:half] == 0, t[1][:half], pltpu.roll(t[2][:half], 64, 1))
    lower = jnp.where(head[half:] == 2, pltpu.roll(t[4][half:], 64, 1), t[5][half:])
    return lo, jnp.where(low[:half], upper, lower)


def kernel(
    seqs, q_hbm, k_hbm, v_hbm, out, q, kbuf, vbuf, weights, column, factor, stats, give, own, got, hop_out, hop_in, mid_out, mid_in, fin, q_sem, k_sem, v_sem,
    stats_send, stats_recv, pair_send, pair_recv, hop_send, hop_recv, mid_send, mid_recv, fin_send, fin_recv,
):
    dp, me = lax.axis_index("dp"), lax.axis_index("sp")
    z, core = me // 2, me % 2
    inner = (z == 1) | (z == 2)
    partner = (dp, z * 2 + (1 - core))
    across = (dp, (3 - z) * 2 + core)
    along = (dp, (z + jnp.where(z % 2 == 0, 1, -1)) * 2 + core)

    def k_copy(s):
        return pltpu.make_async_copy(k_hbm.at[s], kbuf.at[s % DEPTH], k_sem.at[s % DEPTH])

    def v_copy(s):
        return pltpu.make_async_copy(v_hbm.at[s], vbuf.at[s % DEPTH], v_sem.at[s % DEPTH])

    q_copy = pltpu.make_async_copy(q_hbm, q, q_sem)
    q_copy.start()
    for s in range(DEPTH):
        k_copy(s).start()

    barrier = pltpu.get_barrier_semaphore()
    for step in range(1, 8):
        pl.semaphore_signal(barrier, inc=1, device_id=(dp, (me + step) % 8), device_id_type=MESH)
    for s in range(DEPTH):
        v_copy(s).start()
    column[...] = jnp.zeros_like(column)
    q_copy.wait()

    def remote(src, dst, send, recv, device):
        return pltpu.make_async_remote_copy(src_ref=src, dst_ref=dst, send_sem=send, recv_sem=recv, device_id=device, device_id_type=MESH)

    def stats_copy(b, step):
        return remote(stats.at[b, me], stats.at[b, me], stats_send.at[b, step - 1], stats_recv.at[b], (dp, (me + step) % 8))

    def pair_copy(s):
        return remote(give.at[s], got.at[s], pair_send.at[s], pair_recv.at[s], partner)

    def hop_copy(s):
        return remote(hop_out.at[s], hop_in.at[s], hop_send.at[s], hop_recv.at[s], along)

    def mid_copy(s):
        return remote(mid_out.at[s], mid_in.at[s], mid_send.at[s], mid_recv.at[s], across)

    def back_copy(s):
        return remote(fin.at[s, core], fin.at[s, core], hop_send.at[s], hop_recv.at[s], along)

    def fin_copy(s):
        return remote(fin.at[s, core], fin.at[s, core], fin_send.at[s], fin_recv.at[s], partner)

    def score(s):
        k = kbuf.at[s % DEPTH]
        j = s % BATCH
        for half in range(2):
            part = pl.ds(ROWS * half, ROWS)
            scores = jnp.dot(spread(q[s, part, :]), k[pl.ds(WIDE * half, WIDE), :], preferred_element_type=F32)
            high = jnp.max(scores, 1, keepdims=True)
            w = jnp.exp2((scores - high) * RATE)
            weights[s, half] = w.astype(BF16)
            total = jnp.sum(w, 1, keepdims=True)
            lane = lanes((ROWS, 128))
            column[part, :] = jnp.where(lane == j, high, jnp.where(lane == BATCH + j, total, column[part, :]))

    def tell(s):
        @pl.when(s % BATCH == BATCH - 1)
        def _():
            b = s // BATCH
            stats[b, me] = column[...].T[:8]
            for step in range(1, 8):
                stats_copy(b, step).start()

    def learn(s):
        @pl.when(s % BATCH == 0)
        def _():
            b = s // BATCH
            pltpu.make_async_copy(stats.at[b, pl.ds(0, 7)], stats.at[b, pl.ds(0, 7)], stats_recv.at[b]).wait()
            high = functools.reduce(jnp.maximum, [stats[b, d] for d in range(8)])
            total = sum(pltpu.roll(stats[b, d], BATCH, 0) * jnp.exp2((stats[b, d] - high) * RATE) for d in range(8))
            f = jnp.exp2((stats[b, me] - high) * RATE) / total
            factor[...] = jnp.concatenate([f] * 16, 0).T

    def gather(s):
        v = vbuf.at[s % DEPTH]
        lane = lanes((ROWS, 128))
        parts = []
        for half in range(2):
            o = lax.dot_general(weights[s, half], v[pl.ds(WIDE * half, WIDE), :], (((1,), (1,)), ((), ())), preferred_element_type=F32)
            f = jnp.sum(jnp.where(lane == s % BATCH, factor[pl.ds(ROWS * half, ROWS), :], 0.0), 1, keepdims=True)
            parts.append(jnp.concatenate(fold(o * f), 0))
        first = core == 0
        own[s] = jnp.where(first, parts[0], parts[1])
        give[s] = jnp.where(first, parts[1], parts[0]).astype(BF16)

    def inside(s):
        return (s >= 0) & (s < seqs)

    def chip(s):
        @pl.when(inside(s) & jnp.logical_not(inner))
        def _():
            pair_copy(s).wait_recv()
            hop_out[s] = (own[s] + got[s].astype(F32)).astype(BF16)
            hop_copy(s).start()

    def outer(s):
        @pl.when(inside(s) & inner)
        def _():
            pair_copy(s).wait_recv()
            hop_copy(s).wait_recv()
            mid_out[s] = (own[s] + got[s].astype(F32) + hop_in[s].astype(F32)).astype(BF16)
            mid_copy(s).start()

    def middle(s):
        @pl.when(inside(s) & inner)
        def _():
            mid_copy(s).wait_recv()
            fin[s, core] = (mid_out[s].astype(F32) + mid_in[s].astype(F32)).astype(BF16)
            back_copy(s).start()
            fin_copy(s).start()

    def last(s):
        @pl.when(inside(s) & jnp.logical_not(inner))
        def _():
            back_copy(s).wait_recv()
            fin_copy(s).start()

    def result(s):
        @pl.when(inside(s))
        def _():
            fin_copy(s).wait_recv()
            for half in range(2):
                x = fin[s, half].astype(F32)
                tail = jnp.concatenate([x[ROWS:], pltpu.roll(x[ROWS:], 64, 1)], 0)
                out[s, pl.ds(ROWS * half, ROWS), :] = jnp.concatenate([x[:ROWS], tail[:, : HEAD - 128]], 1).astype(BF16)
            pair_copy(s).wait_send()
            hop_copy(s).wait_send()
            fin_copy(s).wait_send()

            @pl.when(inner)
            def _():
                mid_copy(s).wait_send()

    def travel(t):
        chip(t - HOP["chip"])
        outer(t - HOP["outer"])
        middle(t - HOP["middle"])
        last(t - HOP["last"])
        result(t - HOP["out"])

    def head(s, _):
        k_copy(s).wait()
        score(s)
        k_copy(s + DEPTH).start()
        tell(s)

    def both(t, _):
        s = t + LEAD
        learn(t)
        k_copy(s).wait()
        v_copy(t).wait()
        score(s)
        gather(t)
        pair_copy(t).start()

        @pl.when(s + DEPTH < seqs)
        def _():
            k_copy(s + DEPTH).start()

        v_copy(t + DEPTH).start()
        tell(s)
        travel(t)

    def rest(t, _):
        learn(t)
        v_copy(t).wait()
        gather(t)
        pair_copy(t).start()

        @pl.when(t + DEPTH < seqs)
        def _():
            v_copy(t + DEPTH).start()

        travel(t)

    def drain(t, _):
        travel(t)

    def loop(low, high, body):
        lax.fori_loop(low, high, lambda i, carry: (body(i, None), carry)[1], 0)

    pl.semaphore_wait(barrier, 7)
    loop(0, LEAD, head)
    loop(0, seqs - LEAD, both)
    loop(seqs - LEAD, seqs, rest)
    loop(seqs, seqs + HOP["out"], drain)
    for b in range(seqs // BATCH):
        for step in range(1, 8):
            stats_copy(b, step).wait_send()


def attend(q, k, v):
    seqs, tokens = k.shape[:2]
    sem = pltpu.SemaphoreType.DMA
    part = lambda dtype: pltpu.VMEM((seqs, PACK, 128), dtype)
    flat = lambda x: jnp.transpose(x, (0, 2, 3, 1)).reshape(seqs, -1, tokens)
    return pl.pallas_call(
        functools.partial(kernel, seqs),
        out_shape=jax.ShapeDtypeStruct(q.shape, BF16),
        in_specs=[pl.BlockSpec(memory_space=pl.ANY)] * 3,
        out_specs=pl.BlockSpec(memory_space=pltpu.VMEM),
        scratch_shapes=[
            pltpu.VMEM(q.shape, BF16),
            pltpu.VMEM((DEPTH, 2 * WIDE, tokens), BF16),
            pltpu.VMEM((DEPTH, 2 * WIDE, tokens), BF16),
            pltpu.VMEM((seqs, 2, ROWS, tokens), BF16),
            pltpu.VMEM((128, 128), F32),
            pltpu.VMEM((128, 128), F32),
            pltpu.VMEM((seqs // BATCH, 8, 8, 128), F32),
            part(BF16), part(F32), part(BF16), part(BF16), part(BF16), part(BF16), part(BF16),
            pltpu.VMEM((seqs, 2, PACK, 128), BF16),
            sem, sem((DEPTH,)), sem((DEPTH,)),
            sem((seqs // BATCH, 7)), sem((seqs // BATCH,)),
            sem((seqs,)), sem((seqs,)), sem((seqs,)), sem((seqs,)), sem((seqs,)), sem((seqs,)), sem((seqs,)), sem((seqs,)),
        ],
        compiler_params=pltpu.CompilerParams(collective_id=0, has_side_effects=True, vmem_limit_bytes=60 << 20),
    )(q, flat(k), flat(v))


def solution(mesh):
    return jax.shard_map(
        attend,
        mesh=mesh,
        in_specs=(P("dp", None, None), P("dp", "sp", None, None), P("dp", "sp", None, None)),
        out_specs=P("dp", None, None),
        check_vma=False,
    )
```

time: 358 us -> 63 us (0.18)
  waiting for transfers between devices: 223 us -> 0 us
  Pallas kernels: 0 us -> 60.2 us
  matrix products: 41.7 us -> 0 us
  other arithmetic: 40.8 us -> 0 us
  local copies, waits for them, and re-layouts: 37.9 us -> 2.65 us
  between operations: 13.5 us -> 0.01 us
    all_gather x1 -> x0, waiting for transfers between devices: 223 us -> none  [step(): return together(lax.all_gather(part_of(q, k, v), 'sp')).reshape(q.shape)]
    pallas_call x0 -> x1, Pallas kernels: none -> 60.2 us  [attend(): pl.pallas_call(functools.partial(kernel, seqs), out_shape=jax.ShapeDtypeS...]
    dot_general x2 -> x0, matrix products: 41.7 us -> none  [einsum(): return jnp.einsum(form, a.astype(jnp.float32), b.astype(jnp.float32))]
    slice x1 -> x0, other arithmetic: 23.3 us -> none  [together(): seen, total, high = (parts[..., :-2], parts[..., -2:-1], parts[..., -1:])]
    unnamed x6 -> x1, local copies, waits for them, and re-layouts: 23.9 us -> 2.65 us
    reduce_sum x3 -> x0, other arithmetic: 12.9 us -> none  [the longest x1 10.6 us: together(): jnp.sum(seen * scale, 0) / jnp.sum(total * scale, 0)]
    broadcast_in_dim x2 -> x0, local copies, waits for them, and re-layouts: 4.67 us -> none  [the longest x1 3.01 us: part_of(): high = jnp.max(scores, -1, keepdims=True)]
    concatenate x1 -> x0, local copies, waits for them, and re-layouts: 4.61 us -> none  [part_of(): jnp.concatenate([seen, jnp.sum(weights, -1, keepdims=True), high], -1)]
  transfers between devices with their start and end apart: 1 -> 0, of which waited for: 1 -> 0; matrix products, arithmetic and copies ran while one was open for 0% -> 0% of each run, Pallas kernels for 0% -> 0%
where the time goes in v1:
time: 63 us; the launch traced here: 62.9 us
  Pallas kernels  60.2 us (96%)
  local copies, waits for them, and re-layouts  2.65 us (4%)
    pallas_call x1, Pallas kernels, attend(): pl.pallas_call(functools.partial(kernel, seqs), out_shape=jax.ShapeDtypeS...  60.2 us
    unnamed x1, local copies, waits for them, and re-layouts  2.65 us

profile of v1, /device:TPU:0, one launch (start us, length us, event | category | flops | bytes accessed | tf_op | source)
XLA Modules:
  0.0 62.9 jit_solution(6778340845848531372)
XLA Ops:
  0.0 60.2 %shard_map.37 = bf16[32,96,192]{2,1,0:T(8,128)(2,1)} custom-call(bf16[32,96,192]{2,1,0:T(8,128)(2,1)} %q_hbm.1, bf16[32,1536,512]{2,1,0:T(8,128)(2,1)} %bitcast.6, bf16[32,1536,512]{2,1,0:T(8,128)(2,1)} %bitcast.7), custom_call_target="tpu_custom_call" | custom-call | tf_op jit(solution)/shard_map/pallas_call | solution.py:270
  60.2 2.7 %copy.5 = bf16[32,96,192]{2,1,0:T(8,128)(2,1)} copy(bf16[32,96,192]{2,1,0:T(8,128)(2,1)} %shard_map.37) | data formatting | bytes 2359296
